TPU v7x, 32 devices: a whole 2x2x4 slice. The times are simulated.
32 devices in a mesh: clip: 2 (over y), ha: 4 (over z), wa: 4 (over x, core).
Axes of the slice: x: 2, y: 2, z: 4, core: 2. Of those that a mesh axis runs over, the one named last changes fastest.
Arguments:
- cotangent: float32 [8, 16, 256, 96], P('clip', 'ha', 'wa'), parts along dimension 0, may hold values from -6 to 6
- stored_first: float32 [8, 16, 256, 96], P('clip', 'ha', 'wa'), parts along dimension 0, may hold values from -8 to 8
- stored_second: float32 [8, 16, 256, 96], P('clip', 'ha', 'wa'), parts along dimension 0, may hold values from -8 to 8
- w_first: float32 [3, 3, 3, 96, 96], replicated, may hold values from -0.125 to 0.125
- w_second: float32 [3, 3, 3, 96, 96], replicated, may hold values from -0.125 to 0.125
- w_third: float32 [3, 3, 3, 96, 96], replicated, may hold values from -0.125 to 0.125
Outputs:
- input_grad: float32 [8, 16, 256, 96], P('clip', 'ha', 'wa'), parts along dimension 0
There are 2 independent parts, one for each index of `clip`. A program takes and returns all parts, laid end to end along the dimension named above; an argument that names none is the same for every part. Nothing has to cross between parts.
All inputs are finite; a program needn't handle non-finite values.
Results may differ from a plain program's by a relative error of at most 0.00013.
Values sent between devices are 32-bit elements; how exact they have to be, the bound alone decides.
A program may use at most 64 MiB of HBM per device.

v0:
```python
import functools

import jax
import jax.numpy as jnp
from jax import lax
from jax.experimental import pallas as pl
from jax.experimental.pallas import tpu as pltpu
from jax.sharding import PartitionSpec as P

LANES = 128
EDGE = 8
SIDES = tuple((dh, dw) for dh in (-1, 0, 1) for dw in (-1, 0, 1) if (dh, dw) != (0, 0))
COLS = ((0, -1), (0, 1))
ROWS = tuple(s for s in SIDES if s[0] != 0)


def silu_slope(value):
    sigma = 1.0 / (1.0 + jnp.exp(-value))
    return sigma * (1.0 + value * (1.0 - sigma))


def split(value):
    high = value.astype(jnp.bfloat16)
    low = (value - high.astype(jnp.float32)).astype(jnp.bfloat16)
    return high, low


def kernel(
    sizes, cot, first, second, w1, w2, w3, out,
    ext0, ext1, ext2, xs, wbuf0, wbuf1, wbuf2, whl, acc, sfirst, ssecond,
    local_sem, send_sem, recv_sem,
):
    nh, nw, F, R, W, C = sizes
    span = 3 * LANES
    exts = (ext0, ext1, ext2)
    wbufs = (wbuf0, wbuf1, wbuf2)
    ih, iw = lax.axis_index("ha"), lax.axis_index("wa")

    def present(dh, dw):
        ok = ih >= 0
        if dh:
            ok = ok & ((ih > 0) if dh < 0 else (ih < nh - 1))
        if dw:
            ok = ok & ((iw > 0) if dw < 0 else (iw < nw - 1))
        return ok

    def one(flag):
        return jnp.where(flag, jnp.int32(1), jnp.int32(0))

    loads = [
        pltpu.make_async_copy(cot, ext0.at[:, pl.ds(1, R), pl.ds(EDGE, W), :], local_sem.at[0]),
        pltpu.make_async_copy(w3, wbuf0, local_sem.at[1]),
        pltpu.make_async_copy(w2, wbuf1, local_sem.at[2]),
        pltpu.make_async_copy(w1, wbuf2, local_sem.at[3]),
        pltpu.make_async_copy(second, ssecond, local_sem.at[4]),
        pltpu.make_async_copy(first, sfirst, local_sem.at[5]),
    ]
    for load in loads:
        load.start()

    barrier = pltpu.get_barrier_semaphore()
    for dh, dw in SIDES:
        @pl.when(present(dh, dw))
        def _():
            pl.semaphore_signal(
                barrier, inc=1, device_id={"ha": ih + dh, "wa": iw + dw},
                device_id_type=pl.DeviceIdType.MESH,
            )
    tall = 1 + one(ih > 0) + one(ih < nh - 1)
    wide = 1 + one(iw > 0) + one(iw < nw - 1)
    pl.semaphore_wait(barrier, tall * wide - 1)

    def copy_to(phase, dh, dw):
        row, rows = {-1: (0, 1), 0: (0, R), 1: (R - 1, 1)}[dh]
        col, cols = {-1: (0, EDGE), 0: (0, W), 1: (W - EDGE, EDGE)}[dw]
        drow = {-1: R + 1, 0: 1, 1: 0}[dh]
        dcol = {-1: EDGE + W, 0: EDGE, 1: 0}[dw]
        ext = exts[phase]
        if phase == 0:
            src = cot.at[:, pl.ds(row, rows), pl.ds(col, cols), :]
        else:
            src = ext.at[:, pl.ds(row + 1, rows), pl.ds(col + EDGE, cols), :]
        at = SIDES.index((dh, dw))
        return pltpu.make_async_remote_copy(
            src_ref=src,
            dst_ref=ext.at[:, pl.ds(drow, rows), pl.ds(dcol, cols), :],
            send_sem=send_sem.at[phase, at],
            recv_sem=recv_sem.at[phase, at],
            device_id={"ha": ih + dh, "wa": iw + dw},
            device_id_type=pl.DeviceIdType.MESH,
        )

    def send(phase):
        for dh, dw in COLS + ROWS:
            @pl.when(present(dh, dw))
            def _():
                copy_to(phase, dh, dw).start()

    def receive(phase, sides):
        for dh, dw in sides:
            @pl.when(present(-dh, -dw))
            def _():
                copy_to(phase, dh, dw).wait_recv()

    send(0)

    xs[...] = jnp.zeros_like(xs)
    whl[...] = jnp.zeros_like(whl)
    for dh, dw in SIDES:
        @pl.when(jnp.logical_not(present(dh, dw)))
        def _():
            row, rows = {-1: (0, 1), 0: (1, R), 1: (R + 1, 1)}[dh]
            col, cols = {-1: (0, EDGE), 0: (EDGE, W), 1: (EDGE + W, EDGE)}[dw]
            for ext in exts:
                ext[:, row : row + rows, col : col + cols, :] = jnp.zeros(
                    (F, rows, cols, C), jnp.float32
                )

    def prepare(phase):
        wbuf = wbufs[phase]

        @pl.loop(0, 3)
        def _(i):
            for j in range(3):
                for k in range(3):
                    high, low = split(wbuf[i, j, k])
                    whl[i, j, 0:C, k * LANES : k * LANES + C] = high
                    whl[i, j, 0:C, span + k * LANES : span + k * LANES + C] = low

    def arrange(phase, rows):
        ext = exts[phase]

        @pl.loop(0, F)
        def _(f):
            for e in rows:
                for k in range(3):
                    start = EDGE + 1 - k
                    high, low = split(ext[f, e, start : start + W, :])
                    xs[f, e, :, k * LANES : k * LANES + C] = high
                    xs[f, e, :, span + k * LANES : span + k * LANES + C] = low

    pairs = R // 2

    def lhs(i, q):
        shift, frames = 2 - i, F - (2 - i)
        parts = [
            xs[shift : shift + frames, 2 * p + q][:, None] for p in range(pairs)
        ]
        block = jnp.concatenate(parts, axis=1).reshape(frames * pairs * W, 2 * span)
        return jnp.concatenate([block, block[:, :span]], axis=1)

    def rhs(i, j):
        high, low = whl[i, j, :, :span], whl[i, j, :, span:]
        return jnp.concatenate([high, high, low], axis=1)

    def dot(a, b):
        return lax.dot_general(
            a, b, (((1,), (1,)), ((), ())), preferred_element_type=jnp.float32
        )

    def inner():
        for i in (2, 1, 0):
            frames = F - (2 - i)
            a = jnp.concatenate([lhs(i, 1), lhs(i, 2)], axis=1)
            b = jnp.concatenate(
                [
                    jnp.concatenate([rhs(i, 1), rhs(i, 0)], axis=1),
                    jnp.concatenate([rhs(i, 2), rhs(i, 1)], axis=1),
                ],
                axis=0,
            )
            value = dot(a, b).reshape(frames, pairs, W, 2 * LANES)
            if i == 2:
                acc[...] = value
            else:
                acc[0:frames] += value

    def outer():
        for i in (2, 1, 0):
            frames = F - (2 - i)
            for q, j, at in ((0, 2, 0), (3, 0, LANES)):
                value = dot(lhs(i, q), rhs(i, j)).reshape(frames, pairs, W, LANES)
                acc[0:frames, :, :, at : at + LANES] += value

    def result(p, half):
        return acc[:, p, :, half * LANES : half * LANES + C]

    for phase in range(3):
        loads[phase + 1].wait()
        prepare(phase)
        if phase == 0:
            loads[0].wait()
        receive(phase, COLS)
        arrange(phase, range(1, R + 1))
        inner()
        receive(phase, ROWS)
        arrange(phase, (0, R + 1))
        outer()
        if phase < 2:
            loads[4 + phase].wait()
            stored = (ssecond, sfirst)[phase]
            for h in range(R):
                exts[phase + 1][:, h + 1, EDGE : EDGE + W, :] = result(h // 2, h % 2) * silu_slope(
                    stored[:, h]
                )
            send(phase + 1)
        else:
            for h in range(R):
                out[:, h] = result(h // 2, h % 2)

    for phase in range(3):
        for dh, dw in SIDES:
            @pl.when(present(dh, dw))
            def _():
                copy_to(phase, dh, dw).wait_send()


def local(cotangent, stored_first, stored_second, w_first, w_second, w_third):
    F, R, W, C = cotangent.shape
    sizes = (lax.axis_size("ha"), lax.axis_size("wa"), F, R, W, C)
    ext = pltpu.VMEM((F, R + 2, W + 2 * EDGE, C), jnp.float32)
    wbuf = pltpu.VMEM(w_first.shape, jnp.float32)
    stored = pltpu.VMEM((F, R, W, C), jnp.float32)
    return pl.pallas_call(
        functools.partial(kernel, sizes),
        out_shape=jax.ShapeDtypeStruct(cotangent.shape, jnp.float32),
        in_specs=[pl.BlockSpec(memory_space=pl.ANY)] * 6,
        out_specs=pl.BlockSpec(memory_space=pltpu.VMEM),
        scratch_shapes=[
            ext, ext, ext,
            pltpu.VMEM((F, R + 2, W, 6 * LANES), jnp.bfloat16),
            wbuf, wbuf, wbuf,
            pltpu.VMEM((3, 3, LANES, 6 * LANES), jnp.bfloat16),
            pltpu.VMEM((F, R // 2, W, 2 * LANES), jnp.float32),
            stored, stored,
            pltpu.SemaphoreType.DMA((6,)),
            pltpu.SemaphoreType.DMA((3, 8)),
            pltpu.SemaphoreType.DMA((3, 8)),
        ],
        compiler_params=pltpu.CompilerParams(
            collective_id=0, has_side_effects=True, vmem_limit_bytes=48 * 1024 * 1024
        ),
    )(cotangent, stored_first, stored_second, w_first, w_second, w_third)


def solution(mesh):
    split_spec = P("clip", "ha", "wa", None)
    return jax.shard_map(
        local,
        mesh=mesh,
        in_specs=(split_spec, split_spec, split_spec, P(), P(), P()),
        out_specs=split_spec,
        check_vma=False,
    )
```

profile of v0, /device:TPU:1, one launch (start us, length us, event | category | flops | bytes accessed | tf_op | source)
XLA Modules:
  0.0 40.2 jit_solution(9652736416475356382)
XLA Ops:
  0.0 0.0 copy-start
  0.0 1.3 %copy-done = f32[3,3,3,96,96]{4,3,2,1,0:T(8,128)S(1)} copy-done((f32[3,3,3,96,96]{4,3,2,1,0:T(8,128)S(1)}, f32[3,3,3,96,96]{4,3,2,1,0:T(8,128)}, u32[]{:S(2)}) %copy-start) | copy-done | bytes 995352
  1.3 0.0 copy-start.1
  1.3 1.3 %copy-done.1 = f32[3,3,3,96,96]{4,3,2,1,0:T(8,128)S(1)} copy-done((f32[3,3,3,96,96]{4,3,2,1,0:T(8,128)S(1)}, f32[3,3,3,96,96]{4,3,2,1,0:T(8,128)}, u32[]{:S(2)}) %copy-start.1) | copy-done | bytes 995352
  2.6 0.0 copy-start.2
  2.6 1.3 %copy-done.2 = f32[3,3,3,96,96]{4,3,2,1,0:T(8,128)S(1)} copy-done((f32[3,3,3,96,96]{4,3,2,1,0:T(8,128)S(1)}, f32[3,3,3,96,96]{4,3,2,1,0:T(8,128)}, u32[]{:S(2)}) %copy-start.2) | copy-done | bytes 995352
  4.0 0.0 copy-start.3
  4.0 1.0 %copy-done.3 = f32[4,4,64,96]{3,2,1,0:T(8,128)S(1)} copy-done((f32[4,4,64,96]{3,2,1,0:T(8,128)S(1)}, f32[4,4,64,96]{3,2,1,0:T(8,128)}, u32[]{:S(2)}) %copy-start.3) | copy-done | bytes 393240
  5.0 0.0 copy-start.4
  5.0 1.0 %copy-done.4 = f32[4,4,64,96]{3,2,1,0:T(8,128)S(1)} copy-done((f32[4,4,64,96]{3,2,1,0:T(8,128)S(1)}, f32[4,4,64,96]{3,2,1,0:T(8,128)}, u32[]{:S(2)}) %copy-start.4) | copy-done | bytes 393240
  6.1 0.0 copy-start.5
  6.1 1.0 %copy-done.5 = f32[4,4,64,96]{3,2,1,0:T(8,128)S(1)} copy-done((f32[4,4,64,96]{3,2,1,0:T(8,128)S(1)}, f32[4,4,64,96]{3,2,1,0:T(8,128)}, u32[]{:S(2)}) %copy-start.5) | copy-done | bytes 393240
  7.1 32.3 %shard_map.64 = f32[4,4,64,96]{3,2,1,0:T(8,128)S(1)} custom-call(f32[4,4,64,96]{3,2,1,0:T(8,128)S(1)} %copy-done.3, f32[4,4,64,96]{3,2,1,0:T(8,128)S(1)} %copy-done.4, f32[4,4,64,96]{3,2,1,0:T(8,128)S(1)} %copy-done.5, f32[3,3,3,96,96]{4,3,2,1,0:T(8,128)S(1)} %copy-done, f32[3,3,3,96,96]{4,3,2,1,0:T(8,128)S(1)} %copy-done.1, f32[3,3,3,96,96]{4,3,2,1,0:T(8,128)S(1)} %copy-done.2), custom_call_target="tpu_custom_call" | custom-call | tf_op jit(solution)/shard_map/pallas_call | solution.py:224
  39.4 0.8 %copy.8 = f32[4,4,64,96]{3,2,1,0:T(8,128)} copy(f32[4,4,64,96]{3,2,1,0:T(8,128)S(1)} %shard_map.64) | data formatting | bytes 786432
Async XLA Ops:
  0.0 1.3 %copy-start = (f32[3,3,3,96,96]{4,3,2,1,0:T(8,128)S(1)}, f32[3,3,3,96,96]{4,3,2,1,0:T(8,128)}, u32[]{:S(2)}) copy-start(f32[3,3,3,96,96]{4,3,2,1,0:T(8,128)} %w1.1) | copy-start | bytes 2985988
  1.3 1.3 %copy-start.1 = (f32[3,3,3,96,96]{4,3,2,1,0:T(8,128)S(1)}, f32[3,3,3,96,96]{4,3,2,1,0:T(8,128)}, u32[]{:S(2)}) copy-start(f32[3,3,3,96,96]{4,3,2,1,0:T(8,128)} %w2.1) | copy-start | bytes 2985988
  2.6 1.3 %copy-start.2 = (f32[3,3,3,96,96]{4,3,2,1,0:T(8,128)S(1)}, f32[3,3,3,96,96]{4,3,2,1,0:T(8,128)}, u32[]{:S(2)}) copy-start(f32[3,3,3,96,96]{4,3,2,1,0:T(8,128)} %w3.1) | copy-start | bytes 2985988
  4.0 1.0 %copy-start.3 = (f32[4,4,64,96]{3,2,1,0:T(8,128)S(1)}, f32[4,4,64,96]{3,2,1,0:T(8,128)}, u32[]{:S(2)}) copy-start(f32[4,4,64,96]{3,2,1,0:T(8,128)} %cot.1) | copy-start | bytes 1179652
  5.0 1.0 %copy-start.4 = (f32[4,4,64,96]{3,2,1,0:T(8,128)S(1)}, f32[4,4,64,96]{3,2,1,0:T(8,128)}, u32[]{:S(2)}) copy-start(f32[4,4,64,96]{3,2,1,0:T(8,128)} %first.1) | copy-start | bytes 1179652
  6.1 1.0 %copy-start.5 = (f32[4,4,64,96]{3,2,1,0:T(8,128)S(1)}, f32[4,4,64,96]{3,2,1,0:T(8,128)}, u32[]{:S(2)}) copy-start(f32[4,4,64,96]{3,2,1,0:T(8,128)} %second.1) | copy-start | bytes 1179652
where the time goes:
time: 40.5 us; the launch traced here: 40.2 us
  Pallas kernels  32.3 us (80%)
  local copies, waits for them, and re-layouts  7.88 us (19%)
    pallas_call x1, Pallas kernels, local(): pl.pallas_call(functools.partial(kernel, sizes), out_shape=jax.ShapeDtype...  32.3 us
    unnamed x13, local copies, waits for them, and re-layouts  7.88 us

commit v1 on v0

v1 whole, which is shorter than its diff:
```python
import functools

import jax
import jax.numpy as jnp
from jax import lax
from jax.experimental import pallas as pl
from jax.experimental.pallas import tpu as pltpu
from jax.sharding import PartitionSpec as P

LANES = 128
EDGE = 8
SIDES = tuple((dh, dw) for dh in (-1, 0, 1) for dw in (-1, 0, 1) if (dh, dw) != (0, 0))
COLS = ((0, -1), (0, 1))
ROWS = tuple(s for s in SIDES if s[0] != 0)


def silu_slope(value):
    sigma = 1.0 / (1.0 + jnp.exp(-value))
    return sigma * (1.0 + value * (1.0 - sigma))


def split(value):
    high = value.astype(jnp.bfloat16)
    low = (value - high.astype(jnp.float32)).astype(jnp.bfloat16)
    return high, low


def kernel(
    sizes, cot, first, second, w1, w2, w3, out,
    ext0, ext1, ext2, xs, wbuf0, wbuf1, wbuf2, whl, acc, sfirst, ssecond,
    local_sem, send_sem, recv_sem,
):
    nh, nw, F, R, W, C = sizes
    span = 3 * LANES
    exts = (ext0, ext1, ext2)
    wbufs = (wbuf0, wbuf1, wbuf2)
    ih, iw = lax.axis_index("ha"), lax.axis_index("wa")

    def present(dh, dw):
        ok = ih >= 0
        if dh:
            ok = ok & ((ih > 0) if dh < 0 else (ih < nh - 1))
        if dw:
            ok = ok & ((iw > 0) if dw < 0 else (iw < nw - 1))
        return ok

    def one(flag):
        return jnp.where(flag, jnp.int32(1), jnp.int32(0))

    loads = [
        pltpu.make_async_copy(cot, ext0.at[:, pl.ds(1, R), pl.ds(EDGE, W), :], local_sem.at[0]),
        pltpu.make_async_copy(w3, wbuf0, local_sem.at[1]),
        pltpu.make_async_copy(w2, wbuf1, local_sem.at[2]),
        pltpu.make_async_copy(w1, wbuf2, local_sem.at[3]),
        pltpu.make_async_copy(second, ssecond, local_sem.at[4]),
        pltpu.make_async_copy(first, sfirst, local_sem.at[5]),
    ]
    for load in loads:
        load.start()

    barrier = pltpu.get_barrier_semaphore()
    for dh, dw in SIDES:
        @pl.when(present(dh, dw))
        def _():
            pl.semaphore_signal(
                barrier, inc=1, device_id={"ha": ih + dh, "wa": iw + dw},
                device_id_type=pl.DeviceIdType.MESH,
            )
    tall = 1 + one(ih > 0) + one(ih < nh - 1)
    wide = 1 + one(iw > 0) + one(iw < nw - 1)
    pl.semaphore_wait(barrier, tall * wide - 1)

    groups = ((F // 2, F), (0, F // 2))

    def copy_to(phase, group, dh, dw):
        t0, t1 = groups[group]
        row, rows = {-1: (0, 1), 0: (0, R), 1: (R - 1, 1)}[dh]
        col, cols = {-1: (0, EDGE), 0: (0, W), 1: (W - EDGE, EDGE)}[dw]
        drow = {-1: R + 1, 0: 1, 1: 0}[dh]
        dcol = {-1: EDGE + W, 0: EDGE, 1: 0}[dw]
        ext, frames = exts[phase], pl.ds(t0, t1 - t0)
        if phase == 0:
            src = cot.at[frames, pl.ds(row, rows), pl.ds(col, cols), :]
        else:
            src = ext.at[frames, pl.ds(row + 1, rows), pl.ds(col + EDGE, cols), :]
        at = SIDES.index((dh, dw))
        return pltpu.make_async_remote_copy(
            src_ref=src,
            dst_ref=ext.at[frames, pl.ds(drow, rows), pl.ds(dcol, cols), :],
            send_sem=send_sem.at[phase, group, at],
            recv_sem=recv_sem.at[phase, group, at],
            device_id={"ha": ih + dh, "wa": iw + dw},
            device_id_type=pl.DeviceIdType.MESH,
        )

    def send(phase, group):
        for dh, dw in COLS + ROWS:
            @pl.when(present(dh, dw))
            def _():
                copy_to(phase, group, dh, dw).start()

    def receive(phase, group, sides):
        for dh, dw in sides:
            @pl.when(present(-dh, -dw))
            def _():
                copy_to(phase, group, dh, dw).wait_recv()

    send(0, 0)
    send(0, 1)

    xs[...] = jnp.zeros_like(xs)
    for dh, dw in SIDES:
        @pl.when(jnp.logical_not(present(dh, dw)))
        def _():
            row, rows = {-1: (0, 1), 0: (1, R), 1: (R + 1, 1)}[dh]
            col, cols = {-1: (0, EDGE), 0: (EDGE, W), 1: (EDGE + W, EDGE)}[dw]
            for ext in exts:
                ext[:, row : row + rows, col : col + cols, :] = jnp.zeros(
                    (F, rows, cols, C), jnp.float32
                )

    def prepare(phase):
        wbuf = wbufs[phase]

        @pl.loop(0, 3)
        def _(i):
            for j in range(3):
                for k in range(3):
                    turned = split(jnp.transpose(wbuf[i, j, k]))
                    for part in range(2):
                        at = part * span + k * LANES
                        whl[phase, i, j, at : at + C, 0:C] = turned[part]
                        whl[phase, i, j, at + C : at + LANES, :] = jnp.zeros(
                            (LANES - C, LANES), jnp.bfloat16
                        )

    def arrange(phase, group, rows):
        ext = exts[phase]

        @pl.loop(*groups[group])
        def _(f):
            for e in rows:
                for k in range(3):
                    start = EDGE + 1 - k
                    high, low = split(ext[f, e, start : start + W, :])
                    xs[f, e, :, k * LANES : k * LANES + C] = high
                    xs[f, e, :, span + k * LANES : span + k * LANES + C] = low

    pairs = R // 2

    def reach(group, i):
        t0, t1 = groups[group]
        return t0, min(t1, F - 2 + i)

    def lhs(group, i, q):
        t0, t1 = reach(group, i)
        parts = [xs[t0 + 2 - i : t1 + 2 - i, 2 * p + q][:, None] for p in range(pairs)]
        block = jnp.concatenate(parts, axis=1).reshape((t1 - t0) * pairs * W, 2 * span)
        return jnp.concatenate([block, block[:, :span]], axis=1)

    def rhs(phase, i, j):
        high, low = whl[phase, i, j, :span], whl[phase, i, j, span:]
        return jnp.concatenate([high, high, low], axis=0)

    def dot(a, b):
        return jnp.dot(a, b, preferred_element_type=jnp.float32)

    def inner(phase, group):
        for i in (2, 1, 0):
            t0, t1 = reach(group, i)
            if t1 <= t0:
                continue
            a = jnp.concatenate([lhs(group, i, 1), lhs(group, i, 2)], axis=1)
            b = jnp.concatenate(
                [
                    jnp.concatenate([rhs(phase, i, 1), rhs(phase, i, 2)], axis=1),
                    jnp.concatenate([rhs(phase, i, 0), rhs(phase, i, 1)], axis=1),
                ],
                axis=0,
            )
            value = dot(a, b).reshape(t1 - t0, pairs, W, 2 * LANES)
            if i == 2:
                acc[t0:t1] = value
            else:
                acc[t0:t1] += value

    def outer(phase, group):
        for i in (2, 1, 0):
            t0, t1 = reach(group, i)
            if t1 <= t0:
                continue
            for q, j, at in ((0, 2, 0), (3, 0, LANES)):
                value = dot(lhs(group, i, q), rhs(phase, i, j)).reshape(t1 - t0, pairs, W, LANES)
                acc[t0:t1, :, :, at : at + LANES] += value

    for phase in range(3):
        loads[phase + 1].wait()
        prepare(phase)
    loads[0].wait()
    for phase in range(3):
        for group in range(2):
            t0, t1 = groups[group]
            receive(phase, group, COLS)
            arrange(phase, group, range(1, R + 1))
            inner(phase, group)
            receive(phase, group, ROWS)
            arrange(phase, group, (0, R + 1))
            outer(phase, group)
            if phase < 2 and group == 0:
                loads[4 + phase].wait()
            for h in range(R):
                at = h % 2 * LANES
                value = acc[t0:t1, h // 2, :, at : at + C]
                if phase < 2:
                    stored = (ssecond, sfirst)[phase]
                    exts[phase + 1][t0:t1, h + 1, EDGE : EDGE + W, :] = value * silu_slope(
                        stored[t0:t1, h]
                    )
                else:
                    out[t0:t1, h] = value
            if phase < 2:
                send(phase + 1, group)

    for phase in range(3):
        for group in range(2):
            for dh, dw in SIDES:
                @pl.when(present(dh, dw))
                def _():
                    copy_to(phase, group, dh, dw).wait_send()


def local(cotangent, stored_first, stored_second, w_first, w_second, w_third):
    F, R, W, C = cotangent.shape
    sizes = (lax.axis_size("ha"), lax.axis_size("wa"), F, R, W, C)
    ext = pltpu.VMEM((F, R + 2, W + 2 * EDGE, C), jnp.float32)
    wbuf = pltpu.VMEM(w_first.shape, jnp.float32)
    stored = pltpu.VMEM((F, R, W, C), jnp.float32)
    return pl.pallas_call(
        functools.partial(kernel, sizes),
        out_shape=jax.ShapeDtypeStruct(cotangent.shape, jnp.float32),
        in_specs=[pl.BlockSpec(memory_space=pltpu.HBM)] * 6,
        out_specs=pl.BlockSpec(memory_space=pltpu.VMEM),
        scratch_shapes=[
            ext, ext, ext,
            pltpu.VMEM((F, R + 2, W, 6 * LANES), jnp.bfloat16),
            wbuf, wbuf, wbuf,
            pltpu.VMEM((3, 3, 3, 6 * LANES, LANES), jnp.bfloat16),
            pltpu.VMEM((F, R // 2, W, 2 * LANES), jnp.float32),
            stored, stored,
            pltpu.SemaphoreType.DMA((6,)),
            pltpu.SemaphoreType.DMA((3, 2, 8)),
            pltpu.SemaphoreType.DMA((3, 2, 8)),
        ],
        compiler_params=pltpu.CompilerParams(
            collective_id=0, has_side_effects=True, vmem_limit_bytes=67043328
        ),
    )(cotangent, stored_first, stored_second, w_first, w_second, w_third)


def solution(mesh):
    split_spec = P("clip", "ha", "wa", None)
    return jax.shard_map(
        local,
        mesh=mesh,
        in_specs=(split_spec, split_spec, split_spec, P(), P(), P()),
        out_specs=split_spec,
        check_vma=False,
    )
```

time: 40.5 us -> 31.4 us (0.78)
  local copies, waits for them, and re-layouts: 7.88 us -> 1.89 us
  Pallas kernels: 32.3 us -> 29.4 us
    unnamed x13 -> x1, local copies, waits for them, and re-layouts: 7.88 us -> 1.89 us
    pallas_call x1, Pallas kernels: 32.3 us -> 29.4 us  [local(): pl.pallas_call(functools.partial(kernel, sizes), out_shape=jax.ShapeDtype...]
where the time goes in v1:
time: 31.4 us; the launch traced here: 31.3 us
  Pallas kernels  29.4 us (94%)
  local copies, waits for them, and re-layouts  1.89 us (6%)
    pallas_call x1, Pallas kernels, local(): pl.pallas_call(functools.partial(kernel, sizes), out_shape=jax.ShapeDtype...  29.4 us
    unnamed x1, local copies, waits for them, and re-layouts  1.89 us

profile of v1, /device:TPU:1, one launch (start us, length us, event | category | flops | bytes accessed | tf_op | source)
XLA Modules:
  0.0 31.3 jit_solution(1339331358988406002)
XLA Ops:
  0.0 29.4 %shard_map.64 = f32[4,4,64,96]{3,2,1,0:T(8,128)} custom-call(f32[4,4,64,96]{3,2,1,0:T(8,128)} %cot.1, f32[4,4,64,96]{3,2,1,0:T(8,128)} %first.1, f32[4,4,64,96]{3,2,1,0:T(8,128)} %second.1, f32[3,3,3,96,96]{4,3,2,1,0:T(8,128)} %w1.1, f32[3,3,3,96,96]{4,3,2,1,0:T(8,128)} %w2.1, f32[3,3,3,96,96]{4,3,2,1,0:T(8,128)} %w3.1), custom_call_target="tpu_custom_call" | custom-call | tf_op jit(solution)/shard_map/pallas_call | solution.py:238
  29.4 1.9 %copy.8 = f32[4,4,64,96]{3,2,1,0:T(8,128)} copy(f32[4,4,64,96]{3,2,1,0:T(8,128)} %shard_map.64) | data formatting | bytes 786432

commit v2 on v1

--- a/solution.py
+++ b/solution.py
@@ -165,33 +165,29 @@
     def dot(a, b):
         return jnp.dot(a, b, preferred_element_type=jnp.float32)
 
-    def inner(phase, group):
+    def weights(phase, i, j):
+        if 0 <= j <= 2:
+            return rhs(phase, i, j)
+        return jnp.zeros((3 * span, LANES), jnp.bfloat16)
+
+    def multiply(phase, group, offsets, fresh):
         for i in (2, 1, 0):
             t0, t1 = reach(group, i)
             if t1 <= t0:
                 continue
-            a = jnp.concatenate([lhs(group, i, 1), lhs(group, i, 2)], axis=1)
+            a = jnp.concatenate([lhs(group, i, q) for q in offsets], axis=1)
             b = jnp.concatenate(
                 [
-                    jnp.concatenate([rhs(phase, i, 1), rhs(phase, i, 2)], axis=1),
-                    jnp.concatenate([rhs(phase, i, 0), rhs(phase, i, 1)], axis=1),
+                    jnp.concatenate([weights(phase, i, 2 - q), weights(phase, i, 3 - q)], axis=1)
+                    for q in offsets
                 ],
                 axis=0,
             )
             value = dot(a, b).reshape(t1 - t0, pairs, W, 2 * LANES)
-            if i == 2:
+            if fresh and i == 2:
                 acc[t0:t1] = value
             else:
                 acc[t0:t1] += value
-
-    def outer(phase, group):
-        for i in (2, 1, 0):
-            t0, t1 = reach(group, i)
-            if t1 <= t0:
-                continue
-            for q, j, at in ((0, 2, 0), (3, 0, LANES)):
-                value = dot(lhs(group, i, q), rhs(phase, i, j)).reshape(t1 - t0, pairs, W, LANES)
-                acc[t0:t1, :, :, at : at + LANES] += value
 
     for phase in range(3):
         loads[phase + 1].wait()
@@ -200,12 +196,17 @@
     for phase in range(3):
         for group in range(2):
             t0, t1 = groups[group]
-            receive(phase, group, COLS)
-            arrange(phase, group, range(1, R + 1))
-            inner(phase, group)
-            receive(phase, group, ROWS)
-            arrange(phase, group, (0, R + 1))
-            outer(phase, group)
+            if phase and group == 0:
+                receive(phase, group, SIDES)
+                arrange(phase, group, range(R + 2))
+                multiply(phase, group, (0, 1, 2, 3), True)
+            else:
+                receive(phase, group, COLS)
+                arrange(phase, group, range(1, R + 1))
+                multiply(phase, group, (1, 2), True)
+                receive(phase, group, ROWS)
+                arrange(phase, group, (0, R + 1))
+                multiply(phase, group, (0, 3), False)
             if phase < 2 and group == 0:
                 loads[4 + phase].wait()
             for h in range(R):

time: 31.4 us -> 28.7 us (0.914)
  Pallas kernels: 29.4 us -> 26.7 us
    pallas_call x1, Pallas kernels: 29.4 us -> 26.7 us  [local(): pl.pallas_call(functools.partial(kernel, sizes), out_shape=jax.ShapeDtype...]
where the time goes in v2:
time: 28.7 us; the launch traced here: 28.6 us
  Pallas kernels  26.7 us (93%)
  local copies, waits for them, and re-layouts  1.89 us (7%)
    pallas_call x1, Pallas kernels, local(): pl.pallas_call(functools.partial(kernel, sizes), out_shape=jax.ShapeDtype...  26.7 us
    unnamed x1, local copies, waits for them, and re-layouts  1.89 us

profile of v2, /device:TPU:1, one launch (start us, length us, event | category | flops | bytes accessed | tf_op | source)
XLA Modules:
  0.0 28.6 jit_solution(9462631968654528310)
XLA Ops:
  0.0 26.7 %shard_map.64 = f32[4,4,64,96]{3,2,1,0:T(8,128)} custom-call(f32[4,4,64,96]{3,2,1,0:T(8,128)} %cot.1, f32[4,4,64,96]{3,2,1,0:T(8,128)} %first.1, f32[4,4,64,96]{3,2,1,0:T(8,128)} %second.1, f32[3,3,3,96,96]{4,3,2,1,0:T(8,128)} %w1.1, f32[3,3,3,96,96]{4,3,2,1,0:T(8,128)} %w2.1, f32[3,3,3,96,96]{4,3,2,1,0:T(8,128)} %w3.1), custom_call_target="tpu_custom_call" | custom-call | tf_op jit(solution)/shard_map/pallas_call | solution.py:239
  26.7 1.9 %copy.8 = f32[4,4,64,96]{3,2,1,0:T(8,128)} copy(f32[4,4,64,96]{3,2,1,0:T(8,128)} %shard_map.64) | data formatting | bytes 786432
